TPU v7x, 32 devices: a whole 2x2x4 slice. The times are simulated.
32 devices in a mesh: seq: 16 (over z, x, core), chan: 2 (over y).
Axes of the slice: x: 2, y: 2, z: 4, core: 2. Of those that a mesh axis runs over, the one named last changes fastest.
Arguments:
- gate_input: bfloat16 [1024, 4096], P('seq', 'chan'), may hold values from -6 to 6
- key_input: bfloat16 [1024, 4096], P('seq', 'chan'), may hold values from -6 to 6
- value_input: bfloat16 [1024, 4096], P('seq', 'chan'), may hold values from -6 to 6
- decay_rate: float32 [16, 4096], P(None, 'chan'), may hold values from 0.0009765625 to 0.1
- residue: float32 [16, 4096], P(None, 'chan'), may hold values from -1.5 to 1.5
- skip_gain: float32 [4096], P('chan'), may hold values from -3 to 3
- out_weight: bfloat16 [4096, 4096], P('chan', 'seq'), may hold values from -0.125 to 0.125
Outputs:
- mixed: bfloat16 [1024, 4096], P('seq', 'chan')
All inputs are finite; a program needn't handle non-finite values.
Results may differ from a plain program's by a relative error of at most 0.014.
Values may be sent and summed in bfloat16 or wider, within the bound.
A program may use at most 64 MiB of HBM per device.

v0:
```python
import math

import jax
import jax.numpy as jnp
from jax import lax
from jax.sharding import PartitionSpec as P


def phase_table(row_ids, col_ids, modulus, direction):
    turns = row_ids[:, None] * col_ids[None, :] % modulus
    angle = direction * 2.0 * math.pi / modulus * turns.astype(jnp.float32)
    return (jnp.cos(angle), jnp.sin(angle))


def complex_mix(pattern, table, real_part, imag_part):

    def contract(left, right):
        return jnp.einsum(pattern, left, right, precision=lax.Precision.HIGHEST)

    return (
        contract(table[0], real_part) - contract(table[1], imag_part),
        contract(table[0], imag_part) + contract(table[1], real_part),
    )


def complex_times(left_real, left_imag, right_real, right_imag):
    return (
        left_real * right_real - left_imag * right_imag,
        left_real * right_imag + left_imag * right_real,
    )


def transposed_conv(signal, decay_rate, amplitude):
    devices = lax.axis_size("seq")
    seq_index = lax.axis_index("seq")
    row_count, col_count = signal.shape
    own_cols = col_count // devices
    total_rows = row_count * devices
    padded_len = 2 * total_rows
    outer = 2 * devices
    columns = lax.all_to_all(signal, "seq", split_axis=1, concat_axis=0, tiled=True)
    rates = lax.dynamic_slice_in_dim(decay_rate, seq_index * own_cols, own_cols, 1)
    amps = lax.dynamic_slice_in_dim(amplitude, seq_index * own_cols, own_cols, 1)
    positions = jnp.arange(total_rows, dtype=jnp.int32).astype(jnp.float32)

    def add_mode(mode_index, totals):
        return totals + amps[mode_index][None, :] * jnp.exp(
            -rates[mode_index][None, :] * positions[:, None]
        )

    response = lax.fori_loop(
        0, rates.shape[0], add_mode, jnp.zeros((total_rows, own_cols), jnp.float32)
    )
    stacked = jnp.concatenate([columns, response], axis=1)
    shaped = stacked.reshape(row_count // 2, outer, 2 * own_cols)
    half_ids = jnp.arange(row_count // 2, dtype=jnp.int32)
    inner_ids = jnp.arange(row_count, dtype=jnp.int32)
    outer_ids = jnp.arange(outer, dtype=jnp.int32)
    first_table = phase_table(inner_ids, half_ids, row_count, -1.0)
    step_real = jnp.einsum("kn,nac->kac", first_table[0], shaped, precision=lax.Precision.HIGHEST)
    step_imag = jnp.einsum("kn,nac->kac", first_table[1], shaped, precision=lax.Precision.HIGHEST)
    twiddle = phase_table(inner_ids, outer_ids, padded_len, -1.0)
    step_real, step_imag = complex_times(
        step_real, step_imag, twiddle[0][:, :, None], twiddle[1][:, :, None]
    )
    spec_real, spec_imag = complex_mix(
        "ja,kac->kjc", phase_table(outer_ids, outer_ids, outer, -1.0), step_real, step_imag
    )
    prod_real, prod_imag = complex_times(
        spec_real[..., :own_cols],
        spec_imag[..., :own_cols],
        spec_real[..., own_cols:],
        spec_imag[..., own_cols:],
    )
    back_real, back_imag = complex_mix(
        "aj,kjc->kac", phase_table(outer_ids, outer_ids, outer, 1.0), prod_real, prod_imag
    )
    twiddle_back = phase_table(inner_ids, outer_ids, padded_len, 1.0)
    back_real, back_imag = complex_times(
        back_real, back_imag, twiddle_back[0][:, :, None], twiddle_back[1][:, :, None]
    )
    last_table = phase_table(half_ids, inner_ids, row_count, 1.0)
    result = jnp.einsum(
        "mk,kac->mac", last_table[0], back_real, precision=lax.Precision.HIGHEST
    ) - jnp.einsum("mk,kac->mac", last_table[1], back_imag, precision=lax.Precision.HIGHEST)
    convolved_cols = result.reshape(total_rows, own_cols) * (1.0 / padded_len)
    return lax.all_to_all(convolved_cols, "seq", split_axis=0, concat_axis=1, tiled=True)


def body(gate_input, key_input, value_input, decay_rate, residue, skip_gain, out_weight):
    signal = key_input.astype(jnp.float32) * value_input.astype(jnp.float32)
    amplitude = residue * jnp.sqrt(-jnp.expm1(-2.0 * decay_rate))
    convolved = transposed_conv(signal, decay_rate, amplitude)
    gated_rows = (
        gate_input.astype(jnp.float32) * (convolved + skip_gain[None, :] * signal)
    ).astype(jnp.bfloat16)
    partials = jnp.dot(
        gated_rows,
        lax.all_gather(out_weight, "seq", axis=1, tiled=True),
        preferred_element_type=jnp.float32,
    )
    summed = lax.psum_scatter(
        partials.astype(jnp.bfloat16), "chan", scatter_dimension=1, tiled=True
    )
    return summed


def solution(mesh):
    return jax.shard_map(
        body,
        mesh=mesh,
        in_specs=(
            P("seq", "chan"),
            P("seq", "chan"),
            P("seq", "chan"),
            P(None, "chan"),
            P(None, "chan"),
            P("chan"),
            P("chan", "seq"),
        ),
        out_specs=P("seq", "chan"),
        check_vma=False,
    )
```

profile of v0, /device:TPU:7, one launch (start us, length us, event | category | flops | bytes accessed | tf_op | source)
XLA Modules:
  0.0 191.1 jit_solution(2245563752617438048)
XLA Ops:
  6.5 0.0 all-gather.2.cloned.1.call-start
  6.5 0.7 all-gather.2.cloned.1.call-update
  7.3 1.9 copy_bitcast_fusion
  9.2 6.6 %all-to-all-start = ((f32[64,16,128]{2,0,1:T(8,128)}), f32[64,16,128]{2,0,1:T(8,128)S(1)}, u32[]{:S(2)}, u32[]{:S(2)}) async-start(f32[64,16,128]{2,0,1:T(8,128)} %copy_bitcast_fusion), calls=%async_computation | async-start | bytes 1048576 | tf_op jit(solution)/shard_map/all_to_all | solution.py:41
  15.8 0.0 reduce-scatter.2.cloned.1.call-start
  15.9 0.7 constant_dynamic-slice_fusion
  16.6 9.0 %while.14 = (s32[]{:T(128)}, f32[1024,128]{1,0:T(8,128)S(1)}, f32[16,128]{1,0:T(8,128)S(1)}, f32[16,128]{1,0:T(8,128)S(1)}, s32[]{:T(128)}, /*index=5*/s32[]{:T(128)}) while((s32[]{:T(128)}, f32[1024,128]{1,0:T(8,128)S(1)}, f32[16,128]{1,0:T(8,128)S(1)}, f32[16,128]{1,0:T(8,128)S(1)}, s32[]{:T(128)}, /*index=5*/s32[]{:T(128)}) %tuple.40), condition=%wide.region_1.0_spmd.clone, body=%wide.region_0.0_spmd.clone.sunk | while | flops 525443 | bytes 1059923 | solution.py:51
  16.6 0.5 select_add_fusion.2
  17.2 0.5 select_add_fusion.2
  17.8 0.5 select_add_fusion.2
  18.3 0.5 select_add_fusion.2
  18.9 0.5 select_add_fusion.2
  19.5 0.5 select_add_fusion.2
  20.0 0.5 select_add_fusion.2
  20.6 0.5 select_add_fusion.2
  21.2 0.5 select_add_fusion.2
  21.7 0.5 select_add_fusion.2
  22.3 0.5 select_add_fusion.2
  22.8 0.5 select_add_fusion.2
  23.4 0.5 select_add_fusion.2
  24.0 0.5 select_add_fusion.2
  24.5 0.5 select_add_fusion.2
  25.1 0.5 select_add_fusion.2
  25.6 0.1 multiply_cosine_fusion
  25.7 0.1 copy.47
  25.8 0.1 multiply_sine_fusion
  25.9 0.1 copy.48
  26.0 0.1 multiply_sine_fusion.3
  26.1 12.2 %all-to-all-done = f32[64,16,128]{2,0,1:T(8,128)S(1)} async-done(((f32[64,16,128]{2,0,1:T(8,128)}), f32[64,16,128]{2,0,1:T(8,128)S(1)}, u32[]{:S(2)}, u32[]{:S(2)}) %all-to-all-start) | async-done | bytes 524320 | tf_op jit(solution)/shard_map/all_to_all | solution.py:41
  38.2 0.3 copy_dynamic-update-slice_fusion.1
  38.6 0.3 copy_dynamic-update-slice_fusion
  38.9 1.9 %fusion.44 = f32[64,32,256]{2,0,1:T(8,128)S(1)} fusion(f32[32,32,256]{2,0,1:T(8,128)S(1)} %copy_dynamic-update-slice_fusion), kind=kOutput, calls=%fused_computation.70 | convolution fusion | flops 201355264 | bytes 3145728 | tf_op jit(solution)/shard_map/kn,nac->kac/dot_general | solution.py:60
  40.8 2.6 %multiply_subtract_fusion = (f32[64,32,256]{2,0,1:T(8,128)S(1)}, f32[64,32,256]{2,0,1:T(8,128)S(1)}) fusion(f32[64,32,256]{2,0,1:T(8,128)S(1)} %fusion.44, f32[64,32]{0,1:T(8,128)S(1)} %get-tuple-element.135, f32[64,32]{0,1:T(8,128)S(1)} %get-tuple-element.136, f32[32,32,256]{2,0,1:T(8,128)S(1)} %copy_dynamic-update-slice_fusion), kind=kOutput, calls=%fused_computation.9 | convolution fusion | flops 204500992 | bytes 7356416 | tf_op jit(solution)/shard_map/kn,nac->kac/dot_general | solution.py:61
  43.4 3.3 %fusion.4 = f32[64,256,32]{1,2,0:T(8,128)S(1)} fusion(f32[64,32,256]{2,0,1:T(8,128)S(1)} %get-tuple-element.128), kind=kOutput, calls=%fused_computation.12 | convolution fusion | flops 201340928 | bytes 4194304 | tf_op jit(solution)/shard_map/ja,kac->kjc/dot_general | solution.py:18
  46.7 3.3 %fusion.2 = f32[64,256,32]{1,2,0:T(8,128)S(1)} fusion(f32[64,32,256]{2,0,1:T(8,128)S(1)} %get-tuple-element.128), kind=kOutput, calls=%fused_computation.10 | convolution fusion | flops 201340928 | bytes 4194304 | tf_op jit(solution)/shard_map/ja,kac->kjc/dot_general | solution.py:18
  50.0 3.5 %subtract_bitcast_fusion = f32[64,32,256]{2,1,0:T(8,128)S(1)} fusion(f32[64,256,32]{1,2,0:T(8,128)S(1)} %fusion.4, f32[64,32,256]{2,0,1:T(8,128)S(1)} %get-tuple-element.127), kind=kOutput, calls=%fused_computation.7 | convolution fusion | flops 201865216 | bytes 6291456 | tf_op jit(solution)/shard_map/ja,kac->kjc/dot_general | solution.py:18
  53.5 3.3 %add_bitcast_fusion = f32[64,32,256]{2,1,0:T(8,128)S(1)} fusion(f32[64,256,32]{1,2,0:T(8,128)S(1)} %fusion.2, f32[64,32,256]{2,0,1:T(8,128)S(1)} %get-tuple-element.127), kind=kOutput, calls=%fused_computation.6 | convolution fusion | flops 201865216 | bytes 6291456 | tf_op jit(solution)/shard_map/ja,kac->kjc/dot_general | solution.py:18
  56.8 0.3 multiply_subtract_fusion.1
  57.1 1.1 fusion.34
  58.2 1.1 fusion.36
  59.3 1.2 convolution_add_fusion
  60.5 1.6 add_bitcast_fusion.1
  62.1 1.5 fusion.16
  63.6 0.0 copy-start
  63.6 0.0 copy-start.1
  63.6 0.0 copy-start.2
  63.6 0.0 copy-start.3
  63.6 1.3 fusion.14
  64.9 0.3 copy.51
  65.2 36.7 %all_to_all.32 = f32[16,64,128]{2,1,0:T(8,128)S(1)} all-to-all(f32[16,64,128]{2,1,0:T(8,128)S(1)} %bitcast.81), channel_id=1, replica_groups=mesh['seq'=16,'chan'=2] {'seq'}, dimensions={0} | all-to-all | bytes 1048576 | tf_op jit(solution)/shard_map/all_to_all | solution.py:87
  101.9 60.1 %all-gather.2.cloned.1.call-done = bf16[2048,4096]{1,0:T(8,128)(2,1)} async-done(((bf16[2048,256]{1,0:T(8,128)(2,1)}), bf16[2048,4096]{1,0:T(8,128)(2,1)}) %all-gather.2.cloned.1.call-update) | async-done | bytes 16777232 | tf_op jit(solution)/shard_map/all_gather | solution.py:99
  162.0 0.0 copy-done
  162.1 0.0 copy-done.1
  162.1 0.0 copy-done.2
  162.1 0.0 copy-done.3
  162.1 9.6 %convolution_convert_fusion = bf16[64,4096]{1,0:T(8,128)(2,1)} fusion(bf16[2048,4096]{1,0:T(8,128)(2,1)} %all-gather.2.cloned.1.call-done, bf16[64,2048]{1,0:T(8,128)(2,1)S(1)} %copy-done.2, bf16[64,2048]{1,0:T(8,128)(2,1)S(1)} %copy-done, bf16[64,2048]{1,0:T(8,128)(2,1)S(1)} %copy-done.1, f32[2048]{0:T(1024)S(1)} %copy-done.3, ...), kind=kOutput, calls=%fused_computation.5 | convolution fusion | flops 1075052544 | bytes 18620416 | tf_op jit(solution)/shard_map/dot_general | solution.py:97
  171.7 0.0 reduce-scatter.2.cloned.1.call-update
  171.7 12.6 %reduce-scatter.2.cloned.1.call-done = bf16[64,2048]{1,0:T(8,128)(2,1)} async-done(((bf16[64,4096]{1,0:T(8,128)(2,1)}), bf16[64,2048]{1,0:T(8,128)(2,1)}) %reduce-scatter.2.cloned.1.call-update) | async-done | bytes 262160 | tf_op jit(solution)/shard_map/reduce_scatter | solution.py:102
  (33 shorter events, 0.2 us)
Async XLA Ops:
  6.5 155.5 %all-gather.2.cloned.1.call-start = ((), (), s32[]{:S(2)}) async-start(), calls=%async_computation.3 | async-start | bytes 17825792 | tf_op jit(solution)/shard_map/all_gather | solution.py:99
  9.2 29.1 %all-to-all-start = ((f32[64,16,128]{2,0,1:T(8,128)}), f32[64,16,128]{2,0,1:T(8,128)S(1)}, u32[]{:S(2)}, u32[]{:S(2)}) async-start(f32[64,16,128]{2,0,1:T(8,128)} %copy_bitcast_fusion), calls=%async_computation | async-start | bytes 1048576 | tf_op jit(solution)/shard_map/all_to_all | solution.py:41
  15.8 168.5 %reduce-scatter.2.cloned.1.call-start = ((), (), s32[]{:S(2)}) async-start(), calls=%async_computation.4 | async-start | bytes 786432 | tf_op jit(solution)/shard_map/reduce_scatter | solution.py:102
  63.6 98.5 %copy-start = (bf16[64,2048]{1,0:T(8,128)(2,1)S(1)}, bf16[64,2048]{1,0:T(8,128)(2,1)}, u32[]{:S(2)}) copy-start(bf16[64,2048]{1,0:T(8,128)(2,1)} %param.11) | copy-start | bytes 786436
  63.6 98.5 %copy-start.1 = (bf16[64,2048]{1,0:T(8,128)(2,1)S(1)}, bf16[64,2048]{1,0:T(8,128)(2,1)}, u32[]{:S(2)}) copy-start(bf16[64,2048]{1,0:T(8,128)(2,1)} %param.10) | copy-start | bytes 786436
  63.6 98.5 %copy-start.2 = (bf16[64,2048]{1,0:T(8,128)(2,1)S(1)}, bf16[64,2048]{1,0:T(8,128)(2,1)}, u32[]{:S(2)}) copy-start(bf16[64,2048]{1,0:T(8,128)(2,1)} %param.9) | copy-start | bytes 786436
  63.6 98.4 %copy-start.3 = (f32[2048]{0:T(1024)S(1)}, f32[2048]{0:T(1024)}, u32[]{:S(2)}) copy-start(f32[2048]{0:T(1024)} %param.14) | copy-start | bytes 24580
Sparse Core Ops, SparseCore 0:
  9.5 152.5 all-gather.1
  171.8 12.4 reduce-scatter.1
where the time goes:
time: 194 us; the launch traced here: 191 us
  waiting for transfers between devices  85.6 us (44%)
  blocking collectives  36.7 us (19%)
  matrix products  35.1 us (18%)
  between operations  13.6 us (7%)
  other arithmetic  11.6 us (6%)
  starting transfers between devices  6.67 us (3%)
    all_gather x1, waiting for transfers between devices, body(): lax.all_gather(out_weight, 'seq', axis=1, tiled=True)  60.1 us
    all_to_all x1, blocking collectives, transposed_conv(): lax.all_to_all(convolved_cols, 'seq', split_axis=0, concat_axis=1, tiled=...  36.7 us
    dot_general x8, matrix products, contract(): return jnp.einsum(pattern, left, right, precision=lax.Precision.HIGHEST)  18.3 us
    reduce_scatter x1, waiting for transfers between devices, body(): lax.psum_scatter(partials.astype(jnp.bfloat16), 'chan', scatter_dimension...  12.6 us
    all_to_all x1, waiting for transfers between devices, transposed_conv(): lax.all_to_all(signal, 'seq', split_axis=1, concat_axis=0, tiled=True)  12.2 us
    dot_general x1, matrix products, body(): jnp.dot(gated_rows, lax.all_gather(out_weight, 'seq', axis=1, tiled=True)...  9.59 us
    add x16, other arithmetic, add_mode(): totals + amps[mode_index][None, :] * jnp.exp(-rates[mode_index][None, :]...  8.1 us
    all_to_all x1, starting transfers between devices, transposed_conv(): lax.all_to_all(signal, 'seq', split_axis=1, concat_axis=0, tiled=True)  6.63 us
  transfers between devices with their start and end apart: 3, of which 3 were waited for; matrix products, arithmetic and copies ran while one was open for 20% of the time, Pallas kernels for 0%

commit v1 on v0

v1 whole, which is shorter than its diff:
```python
import functools

import jax
import jax.numpy as jnp
from jax import lax
from jax.experimental import pallas as pl
from jax.experimental.pallas import tpu as pltpu
from jax.sharding import PartitionSpec as P

MESH = pl.DeviceIdType.MESH
F32 = jnp.float32
BF16 = jnp.bfloat16
LANES = 128
SUB = 8


def kernel(
    n, n_chan,
    q_ref, k_ref, v_ref, rate_ref, amp_ref, skip_ref, w_ref, out_ref,
    sig, local, padded, fades, ends, ends_all, starts_all, starts, gathered, partial, landed,
    end_send, end_recv, start_send, start_recv, gather_send, gather_recv, part_send, part_recv,
):
    tok, chans = q_ref.shape
    modes = rate_ref.shape[0]
    blocks = chans // LANES
    rows = modes * blocks // n
    per_block = modes // rows
    width = w_ref.shape[1]
    per_chan = n // n_chan
    ring = n // 4
    tiles = tok // SUB

    me = lax.axis_index("seq")
    chan = lax.axis_index("chan")
    z = me // 4
    x = (me // 2) % 2
    c = me % 2
    steps = lax.broadcasted_iota(jnp.int32, (SUB, LANES), 0).astype(F32)

    def lanes(b):
        return pl.ds(pl.multiple_of(b * LANES, LANES), LANES)

    def end_block(b, _):
        at = lanes(b)
        s = k_ref[:, at].astype(F32) * v_ref[:, at].astype(F32)
        sig[:, at] = s
        found = []
        for m in range(modes):
            rate = rate_ref[pl.ds(m, 1), at]
            jump = jnp.exp(-float(SUB) * rate)
            total = s[:SUB]
            for t in range(1, tiles):
                total = total * jump + s[t * SUB:(t + 1) * SUB]
            total = total * jnp.exp(-rate * (float(SUB - 1) - steps))
            found.append(jnp.sum(total, axis=0, keepdims=True))
        state = jnp.concatenate(found, axis=0)
        fade = jnp.exp(-float(tok) * rate_ref[:, at])
        for p in range(per_block):
            ends[b * per_block + p] = state[p * rows:(p + 1) * rows]
            fades[b * per_block + p] = fade[p * rows:(p + 1) * rows]
        return 0

    lax.fori_loop(0, blocks, end_block, 0)

    def exchange(source, target, send_sem, recv_sem):
        copies = []
        for hop in range(1, n):
            peer = lax.rem(me + hop, n)
            copy = pltpu.make_async_remote_copy(
                src_ref=source.at[peer], dst_ref=target.at[me],
                send_sem=send_sem.at[hop], recv_sem=recv_sem.at[me],
                device_id=(peer, chan), device_id_type=MESH,
            )
            copy.start()
            copies.append(copy)
        target[me] = source[me]
        return copies

    def arrivals(target, send_sem, recv_sem):
        for hop in range(1, n):
            peer = lax.rem(me + hop, n)
            pltpu.make_async_remote_copy(
                src_ref=target.at[peer], dst_ref=target.at[peer],
                send_sem=send_sem.at[hop], recv_sem=recv_sem.at[peer],
                device_id=(peer, chan), device_id_type=MESH,
            ).wait_recv()

    end_copies = exchange(ends, ends_all, end_send, end_recv)

    padded[:SUB] = jnp.zeros((SUB, LANES), F32)

    def local_block(b, _):
        at = lanes(b)
        response = [jnp.zeros((SUB, LANES), F32)] * tiles
        for m in range(modes):
            rate = rate_ref[pl.ds(m, 1), at]
            jump = jnp.exp(-float(SUB) * rate)
            term = amp_ref[pl.ds(m, 1), at] * jnp.exp(-rate * steps)
            for t in range(tiles):
                response[t] = response[t] + term
                if t < tiles - 1:
                    term = term * jump
        padded[SUB:] = jnp.concatenate(response, axis=0)
        skip = skip_ref[:, at]
        totals = [skip * sig[t * SUB:(t + 1) * SUB, at] for t in range(tiles)]
        for lag in range(SUB):
            moved = [padded[pl.ds(SUB - lag + t * SUB, SUB)] for t in range(tiles)]
            for first in range(tiles):
                value = sig[pl.ds(first * SUB + lag, 1), at]
                for t in range(first, tiles):
                    totals[t] = totals[t] + moved[t - first] * value
        for t in range(tiles):
            local[t * SUB:(t + 1) * SUB, at] = totals[t]
        return 0

    lax.fori_loop(0, blocks, local_block, 0)

    arrivals(ends_all, end_send, end_recv)
    fade = fades[me]
    state = jnp.zeros((rows, LANES), F32)
    for i in range(n):
        starts_all[i] = state
        if i < n - 1:
            state = state * fade + ends_all[i]
    start_copies = exchange(starts_all, starts, start_send, start_recv)
    arrivals(starts, start_send, start_recv)

    own_rows = pl.multiple_of(me * tok, tok)

    def gate_block(b, _):
        at = lanes(b)
        totals = [local[t * SUB:(t + 1) * SUB, at] for t in range(tiles)]
        for m in range(modes):
            rate = rate_ref[pl.ds(m, 1), at]
            jump = jnp.exp(-float(SUB) * rate)
            start = starts[b * per_block + m // rows][m % rows:m % rows + 1]
            term = (amp_ref[pl.ds(m, 1), at] * start) * jnp.exp(-rate * (steps + 1.0))
            for t in range(tiles):
                totals[t] = totals[t] + term
                if t < tiles - 1:
                    term = term * jump
        gated = q_ref[:, at].astype(F32) * jnp.concatenate(totals, axis=0)
        gathered[pl.ds(own_rows, tok), at] = gated.astype(BF16)
        return 0

    lax.fori_loop(0, blocks, gate_block, 0)

    half_rows = tok // 2
    sib = me + 1 - 2 * c
    across = me + 2 - 4 * x
    right = lax.rem(me + 4, n)
    left = lax.rem(me + n - 4, n)
    sent = []

    def slot_of(dz, dx, dc):
        return lax.rem(z + dz + ring, ring) * 4 + (x + dx - 2 * x * dx) * 2 + (c + dc - 2 * c * dc)

    def piece(half, slot):
        return gathered.at[pl.ds(pl.multiple_of(slot * tok + half * half_rows, half_rows), half_rows)]

    def send(half, slot, peer):
        copy = pltpu.make_async_remote_copy(
            src_ref=piece(half, slot), dst_ref=piece(half, slot),
            send_sem=gather_send.at[len(sent)], recv_sem=gather_recv.at[half * n + slot],
            device_id=(peer, chan), device_id_type=MESH,
        )
        copy.start()
        sent.append(copy)

    def receive(half, slot):
        pltpu.make_async_remote_copy(
            src_ref=piece(half, slot), dst_ref=piece(half, slot),
            send_sem=gather_send.at[0], recv_sem=gather_recv.at[half * n + slot],
            device_id=(sib, chan), device_id_type=MESH,
        ).wait_recv()

    def goes_on(half, d, to_right):
        far = (half == 0) == to_right
        return 2 * (d + 1) <= ring if far else 2 * (d + 1) < ring

    def pass_on(half, slot, d, go_right, go_left):
        if go_right and goes_on(half, d, True):
            send(half, slot, right)
        if go_left and goes_on(half, d, False):
            send(half, slot, left)

    out_chan = me // per_chan
    part_waits = []

    def project(dz):
        base = lax.rem(z + dz + ring, ring) * 4
        at = pl.ds(pl.multiple_of(base * tok, 4 * tok), 4 * tok)
        partial[at] = jnp.dot(
            gathered[at], w_ref[...], preferred_element_type=F32
        ).astype(BF16)
        for q in range(4):
            to = base + q
            source = partial.at[pl.ds(pl.multiple_of(to * tok, tok), tok)]
            slot = chan * per_chan + lax.rem(me, per_chan)
            copy = pltpu.make_async_remote_copy(
                src_ref=source, dst_ref=landed.at[slot],
                send_sem=part_send.at[len(part_waits)], recv_sem=part_recv.at[slot],
                device_id=(to, out_chan), device_id_type=MESH,
            )
            here = None
            if dz == 0:
                here = jnp.logical_and(to == me, out_chan == chan)

                @pl.when(here)
                def _():
                    pltpu.make_async_copy(source, landed.at[slot], part_recv.at[slot]).start()

                @pl.when(jnp.logical_not(here))
                def _():
                    copy.start()
            else:
                copy.start()
            part_waits.append((here, copy))

    send(0, me, across)
    pass_on(1, me, 0, True, True)
    pass_on(0, me, 0, True, True)
    send(1, me, across)
    for half in range(2):
        send(half, me, sib)
    other = slot_of(0, 1, 0)
    receive(0, other)
    pass_on(0, other, 0, True, True)
    send(0, other, sib)
    receive(1, other)
    send(1, other, sib)
    for half in range(2):
        for dx in range(2):
            receive(half, slot_of(0, dx, 1))
    project(0)
    d = 1
    while 2 * d <= ring:
        planes = []
        for to_right in (True, False):
            dz = -d if to_right else d
            for half in range(2):
                if not goes_on(half, d - 1, to_right):
                    continue
                for dx in range(2 if half == 0 else 1):
                    slot = slot_of(dz, dx, 0)
                    receive(half, slot)
                    pass_on(half, slot, d, to_right, not to_right)
                    if half == 1:
                        send(1, slot, across)
                    send(half, slot, sib)
            if not planes or 2 * d < ring:
                planes.append(dz)
        for dz in planes:
            slot = slot_of(dz, 1, 0)
            receive(1, slot)
            send(1, slot, sib)
        for dz in planes:
            for half in range(2):
                for dx in range(2):
                    receive(half, slot_of(dz, dx, 1))
            project(dz)
        d += 1

    for i in range(per_chan):
        total = None
        for j in range(n_chan):
            slot = j * per_chan + i
            pltpu.make_async_remote_copy(
                src_ref=landed.at[slot], dst_ref=landed.at[slot],
                send_sem=part_send.at[0], recv_sem=part_recv.at[slot],
                device_id=(sib, chan), device_id_type=MESH,
            ).wait_recv()
            part = landed[slot].astype(F32)
            total = part if total is None else total + part
        out_ref[:, i * width:(i + 1) * width] = total.astype(BF16)

    for copy in end_copies + start_copies + sent:
        copy.wait_send()
    for here, copy in part_waits:
        if here is None:
            copy.wait_send()
        else:
            @pl.when(jnp.logical_not(here))
            def _():
                copy.wait_send()


def solution(mesh):
    n, n_chan = mesh.shape["seq"], mesh.shape["chan"]
    assert n % 4 == 0 and n % n_chan == 0

    def body(gate_input, key_input, value_input, decay_rate, residue, skip_gain, out_weight):
        tok, chans = gate_input.shape
        modes = decay_rate.shape[0]
        width = out_weight.shape[1]
        rows = modes * chans // (LANES * n)
        amplitude = residue * jnp.sqrt(-jnp.expm1(-2.0 * decay_rate))
        vmem = pl.BlockSpec(memory_space=pltpu.VMEM)
        dma = pltpu.SemaphoreType.DMA
        states = pltpu.VMEM((n, rows, LANES), F32)
        return pl.pallas_call(
            functools.partial(kernel, n, n_chan),
            out_shape=jax.ShapeDtypeStruct((tok, width * (n // n_chan)), BF16),
            in_specs=[vmem] * 7,
            out_specs=vmem,
            scratch_shapes=[
                pltpu.VMEM((tok, chans), F32),
                pltpu.VMEM((tok, chans), F32),
                pltpu.VMEM((tok + SUB, LANES), F32),
                states, states, states, states, states,
                pltpu.VMEM((n * tok, chans), BF16),
                pltpu.VMEM((n * tok, width), BF16),
                pltpu.VMEM((n, tok, width), BF16),
                dma((n,)), dma((n,)), dma((n,)), dma((n,)),
                dma((8 * n,)), dma((2 * n,)), dma((n,)), dma((n,)),
            ],
            compiler_params=pltpu.CompilerParams(
                has_side_effects=True, vmem_limit_bytes=48 * 1024 * 1024
            ),
            cost_estimate=pl.CostEstimate(
                flops=2 * n * tok * chans * width, bytes_accessed=4 * tok * chans, transcendentals=0
            ),
        )(gate_input, key_input, value_input, decay_rate, amplitude,
          skip_gain.reshape(1, chans), out_weight)

    return jax.shard_map(
        body,
        mesh=mesh,
        in_specs=(
            P("seq", "chan"),
            P("seq", "chan"),
            P("seq", "chan"),
            P(None, "chan"),
            P(None, "chan"),
            P("chan"),
            P("chan", "seq"),
        ),
        out_specs=P("seq", "chan"),
        check_vma=False,
    )
```

time: 194 us -> 72.6 us (0.37); the launches traced: 191 us -> 72.3 us
  waiting for transfers between devices: 85.6 us -> 0 us
  Pallas kernels: 0 us -> 66.7 us
  blocking collectives: 36.7 us -> 0 us
  matrix products: 35.1 us -> 0 us
  between operations: 13.6 us -> 0.04 us
  other arithmetic: 11.6 us -> 1.11 us
  starting transfers between devices: 6.67 us -> 0 us
  local copies, waits for them, and re-layouts: 1.11 us -> 4.53 us
    pallas_call x0 -> x1, Pallas kernels: none -> 66.7 us  [body(): pl.pallas_call(functools.partial(kernel, n, n_chan), out_shape=jax.ShapeD...]
    all_gather x1 -> x0, waiting for transfers between devices: 60.1 us -> none  [body(): lax.all_gather(out_weight, 'seq', axis=1, tiled=True)]
    all_to_all x1 -> x0, blocking collectives: 36.7 us -> none  [transposed_conv(): lax.all_to_all(convolved_cols, 'seq', split_axis=0, concat_axis=1, tiled=...]
    dot_general x13 -> x0, matrix products: 35.1 us -> none  [the longest x8 18.3 us: contract(): return jnp.einsum(pattern, left, right, precision=lax.Precision.HIGHEST)]
    reduce_scatter x1 -> x0, waiting for transfers between devices: 12.6 us -> none  [body(): lax.psum_scatter(partials.astype(jnp.bfloat16), 'chan', scatter_dimension...]
    all_to_all x1 -> x0, waiting for transfers between devices: 12.2 us -> none  [transposed_conv(): lax.all_to_all(signal, 'seq', split_axis=1, concat_axis=0, tiled=True)]
    add x16 -> x0, other arithmetic: 8.1 us -> none  [add_mode(): totals + amps[mode_index][None, :] * jnp.exp(-rates[mode_index][None, :]...]
    all_to_all x1 -> x0, starting transfers between devices: 6.63 us -> none  [transposed_conv(): lax.all_to_all(signal, 'seq', split_axis=1, concat_axis=0, tiled=True)]
  transfers between devices with their start and end apart: 3 -> 0, of which waited for: 3 -> 0; matrix products, arithmetic and copies ran while one was open for 20% -> 0% of each run, Pallas kernels for 0% -> 0%
where the time goes in v1:
time: 72.6 us; the launch traced here: 72.3 us
  Pallas kernels  66.7 us (92%)
  local copies, waits for them, and re-layouts  4.53 us (6%)
  other arithmetic  1.11 us (2%)
    pallas_call x1, Pallas kernels, body(): pl.pallas_call(functools.partial(kernel, n, n_chan), out_shape=jax.ShapeD...  66.7 us
    unnamed x13, local copies, waits for them, and re-layouts  4.53 us

profile of v1, /device:TPU:7, one launch (start us, length us, event | category | flops | bytes accessed | tf_op | source)
XLA Modules:
  0.0 72.3 jit_solution(12409657011629915495)
XLA Ops:
  0.0 0.0 copy-start.2
  0.0 0.0 copy-start
  0.0 1.1 %sqrt_multiply_fusion.amp_ref = f32[16,2048]{1,0:T(8,128)S(1)} fusion(f32[16,2048]{1,0:T(8,128)} %param.11, f32[16,2048]{1,0:T(8,128)} %rate_ref.1), kind=kLoop, calls=%fused_computation | loop fusion | flops 98304 | bytes 393216 | tf_op jit(solution)/shard_map/mul | solution.py:297
  1.1 0.0 copy-done.2
  1.1 0.0 copy-done
  1.1 0.0 copy-start.1
  1.1 1.2 %copy-done.1 = bf16[2048,256]{1,0:T(8,128)(2,1)S(1)} copy-done((bf16[2048,256]{1,0:T(8,128)(2,1)S(1)}, bf16[2048,256]{1,0:T(8,128)(2,1)}, u32[]{:S(2)}) %copy-start.1) | copy-done | bytes 1048600
  2.4 0.0 copy-start.3
  2.4 0.9 %copy-done.3 = bf16[64,2048]{1,0:T(8,128)(2,1)S(1)} copy-done((bf16[64,2048]{1,0:T(8,128)(2,1)S(1)}, bf16[64,2048]{1,0:T(8,128)(2,1)}, u32[]{:S(2)}) %copy-start.3) | copy-done | bytes 262168
  3.3 0.0 copy-start.4
  3.3 0.9 %copy-done.4 = bf16[64,2048]{1,0:T(8,128)(2,1)S(1)} copy-done((bf16[64,2048]{1,0:T(8,128)(2,1)S(1)}, bf16[64,2048]{1,0:T(8,128)(2,1)}, u32[]{:S(2)}) %copy-start.4) | copy-done | bytes 262168
  4.3 0.0 copy-start.5
  4.3 0.7 copy-done.5
  5.0 66.7 %shard_map.73 = bf16[64,2048]{1,0:T(8,128)(2,1)S(1)} custom-call(bf16[64,2048]{1,0:T(8,128)(2,1)S(1)} %copy-done.2, bf16[64,2048]{1,0:T(8,128)(2,1)S(1)} %copy-done.3, bf16[64,2048]{1,0:T(8,128)(2,1)S(1)} %copy-done.4, f32[16,2048]{1,0:T(8,128)S(1)} %copy-done, f32[16,2048]{1,0:T(8,128)S(1)} %sqrt_multiply_fusion.amp_ref, f32[1,2048]{1,0:T(1,128)S(1)} %bitcast.1, ...), custom_call_target="tpu_custom_call" | custom-call | flops 1073741824 | bytes 524288 | tf_op jit(solution)/shard_map/pallas_call | solution.py:301
  71.6 0.7 copy.9
Async XLA Ops:
  0.0 1.1 %copy-start.2 = (bf16[64,2048]{1,0:T(8,128)(2,1)S(1)}, bf16[64,2048]{1,0:T(8,128)(2,1)}, u32[]{:S(2)}) copy-start(bf16[64,2048]{1,0:T(8,128)(2,1)} %q_ref.1) | copy-start | bytes 786436
  0.0 1.1 %copy-start = (f32[16,2048]{1,0:T(8,128)S(1)}, f32[16,2048]{1,0:T(8,128)}, u32[]{:S(2)}) copy-start(f32[16,2048]{1,0:T(8,128)} %rate_ref.1) | copy-start | bytes 393220
  1.1 1.2 %copy-start.1 = (bf16[2048,256]{1,0:T(8,128)(2,1)S(1)}, bf16[2048,256]{1,0:T(8,128)(2,1)}, u32[]{:S(2)}) copy-start(bf16[2048,256]{1,0:T(8,128)(2,1)} %w_ref.1) | copy-start | bytes 3145732
  2.4 0.9 %copy-start.3 = (bf16[64,2048]{1,0:T(8,128)(2,1)S(1)}, bf16[64,2048]{1,0:T(8,128)(2,1)}, u32[]{:S(2)}) copy-start(bf16[64,2048]{1,0:T(8,128)(2,1)} %k_ref.1) | copy-start | bytes 786436
  3.3 0.9 %copy-start.4 = (bf16[64,2048]{1,0:T(8,128)(2,1)S(1)}, bf16[64,2048]{1,0:T(8,128)(2,1)}, u32[]{:S(2)}) copy-start(bf16[64,2048]{1,0:T(8,128)(2,1)} %v_ref.1) | copy-start | bytes 786436
  4.3 0.7 copy-start.5

commit v2 on v1

v2 whole, which is shorter than its diff:
```python
import functools

import jax
import jax.numpy as jnp
from jax import lax
from jax.experimental import pallas as pl
from jax.experimental.pallas import tpu as pltpu
from jax.sharding import PartitionSpec as P

MESH = pl.DeviceIdType.MESH
F32 = jnp.float32
BF16 = jnp.bfloat16
LANES = 128
SUB = 8


def one_minus_exp(y):
    series = jnp.ones_like(y)
    for order in range(10, 1, -1):
        series = 1.0 - y * (1.0 / order) * series
    return jnp.where(y < 0.4, y * series, 1.0 - jnp.exp(-y))


def kernel(
    n, n_chan,
    q_hbm, k_hbm, v_hbm, rate_hbm, residue_hbm, skip_ref, w_hbm, out_ref,
    q_ref, k_ref, v_ref, rate_ref, amp_ref, w_ref, w_other, load_sem, w_send, w_recv,
    sig, local, padded, fades, ends, ends_all, starts_all, starts, gathered, partial, landed,
    end_send, end_recv, start_send, start_recv, gather_send, gather_recv, part_send, part_recv,
):
    loads = [
        pltpu.make_async_copy(source, target, load_sem.at[i])
        for i, (source, target) in enumerate([
            (k_hbm, k_ref), (v_hbm, v_ref), (rate_hbm, rate_ref),
            (residue_hbm, amp_ref), (q_hbm, q_ref), (w_hbm, w_ref),
        ])
    ]
    for load in loads:
        load.start()
    tok, chans = q_ref.shape
    modes = rate_ref.shape[0]
    blocks = chans // LANES
    rows = modes * blocks // n
    per_block = modes // rows
    width = w_ref.shape[1]
    per_chan = n // n_chan
    line = n // 4
    tiles = tok // SUB

    me = lax.axis_index("seq")
    chan = lax.axis_index("chan")
    z = me // 4
    x = (me // 2) % 2
    c = me % 2
    barrier = pltpu.get_barrier_semaphore()
    for hop in range(1, n):
        pl.semaphore_signal(
            barrier, inc=1, device_id=(lax.rem(me + hop, n), chan), device_id_type=MESH
        )
    for turn in range(1, n_chan):
        for slot in range(2 * line):
            peer = (slot // 2) * 4 + x * 2 + slot % 2
            pl.semaphore_signal(
                barrier, inc=1, device_id=(peer, lax.rem(chan + turn, n_chan)), device_id_type=MESH
            )
    steps = lax.broadcasted_iota(jnp.int32, (SUB, LANES), 0).astype(F32)

    def lanes(b):
        return pl.ds(pl.multiple_of(b * LANES, LANES), LANES)

    for load in loads[:3]:
        load.wait()

    def end_block(b, _):
        at = lanes(b)
        s = k_ref[:, at].astype(F32) * v_ref[:, at].astype(F32)
        sig[:, at] = s
        found = []
        for m in range(modes):
            rate = rate_ref[pl.ds(m, 1), at]
            jump = jnp.exp(-float(SUB) * rate)
            total = s[:SUB]
            for t in range(1, tiles):
                total = total * jump + s[t * SUB:(t + 1) * SUB]
            total = total * jnp.exp(-rate * (float(SUB - 1) - steps))
            found.append(jnp.sum(total, axis=0, keepdims=True))
        state = jnp.concatenate(found, axis=0)
        fade = jnp.exp(-float(tok) * rate_ref[:, at])
        for p in range(per_block):
            ends[b * per_block + p] = state[p * rows:(p + 1) * rows]
            fades[b * per_block + p] = fade[p * rows:(p + 1) * rows]
        return 0

    lax.fori_loop(0, blocks, end_block, 0)

    pl.semaphore_wait(barrier, n - 1 + (n_chan - 1) * 2 * line)

    def exchange(source, target, send_sem, recv_sem):
        copies = []
        for hop in range(1, n):
            peer = lax.rem(me + hop, n)
            copy = pltpu.make_async_remote_copy(
                src_ref=source.at[peer], dst_ref=target.at[me],
                send_sem=send_sem.at[hop], recv_sem=recv_sem.at[me],
                device_id=(peer, chan), device_id_type=MESH,
            )
            copy.start()
            copies.append(copy)
        target[me] = source[me]
        return copies

    def arrivals(target, send_sem, recv_sem):
        for hop in range(1, n):
            peer = lax.rem(me + hop, n)
            pltpu.make_async_remote_copy(
                src_ref=target.at[peer], dst_ref=target.at[peer],
                send_sem=send_sem.at[hop], recv_sem=recv_sem.at[peer],
                device_id=(peer, chan), device_id_type=MESH,
            ).wait_recv()

    end_copies = exchange(ends, ends_all, end_send, end_recv)

    loads[3].wait()
    amp_ref[...] = amp_ref[...] * jnp.sqrt(one_minus_exp(2.0 * rate_ref[...]))

    padded[:SUB] = jnp.zeros((SUB, LANES), F32)

    def local_block(b, _):
        at = lanes(b)
        response = [jnp.zeros((SUB, LANES), F32)] * tiles
        for m in range(modes):
            rate = rate_ref[pl.ds(m, 1), at]
            jump = jnp.exp(-float(SUB) * rate)
            term = amp_ref[pl.ds(m, 1), at] * jnp.exp(-rate * steps)
            for t in range(tiles):
                response[t] = response[t] + term
                if t < tiles - 1:
                    term = term * jump
        padded[SUB:] = jnp.concatenate(response, axis=0)
        skip = skip_ref[:, at]
        totals = [skip * sig[t * SUB:(t + 1) * SUB, at] for t in range(tiles)]
        for lag in range(SUB):
            moved = [padded[pl.ds(SUB - lag + t * SUB, SUB)] for t in range(tiles)]
            for first in range(tiles):
                value = sig[pl.ds(first * SUB + lag, 1), at]
                for t in range(first, tiles):
                    totals[t] = totals[t] + moved[t - first] * value
        for t in range(tiles):
            local[t * SUB:(t + 1) * SUB, at] = totals[t]
        return 0

    lax.fori_loop(0, blocks, local_block, 0)

    arrivals(ends_all, end_send, end_recv)
    fade = fades[me]
    state = jnp.zeros((rows, LANES), F32)
    for i in range(n):
        starts_all[i] = state
        if i < n - 1:
            state = state * fade + ends_all[i]
    start_copies = exchange(starts_all, starts, start_send, start_recv)
    across = me + 2 - 4 * x
    w_copies = []
    w_rows = chans // 2
    for half in range(2):
        at = pl.ds(half * w_rows, w_rows)
        copy = pltpu.make_async_remote_copy(
            src_ref=w_hbm.at[at], dst_ref=w_other.at[at],
            send_sem=w_send.at[half], recv_sem=w_recv.at[half],
            device_id=(across, chan), device_id_type=MESH,
        )
        copy.start()
        w_copies.append(copy)
    loads[4].wait()
    arrivals(starts, start_send, start_recv)

    own_rows = pl.multiple_of((2 * z + c) * tok, tok)

    def gate_block(b, _):
        at = lanes(b)
        totals = [local[t * SUB:(t + 1) * SUB, at] for t in range(tiles)]
        for m in range(modes):
            rate = rate_ref[pl.ds(m, 1), at]
            jump = jnp.exp(-float(SUB) * rate)
            start = starts[b * per_block + m // rows][m % rows:m % rows + 1]
            term = (amp_ref[pl.ds(m, 1), at] * start) * jnp.exp(-rate * (steps + 1.0))
            for t in range(tiles):
                totals[t] = totals[t] + term
                if t < tiles - 1:
                    term = term * jump
        gated = q_ref[:, at].astype(F32) * jnp.concatenate(totals, axis=0)
        gathered[pl.ds(own_rows, tok), at] = gated.astype(BF16)
        return 0

    lax.fori_loop(0, blocks, gate_block, 0)

    half_rows = tok // 2
    sib = me + 1 - 2 * c
    has_right = z < line - 1
    has_left = z > 0
    sent = []

    def piece(half, slot):
        return gathered.at[pl.ds(pl.multiple_of(slot * tok + half * half_rows, half_rows), half_rows)]

    def send(half, slot, peer, cond):
        copy = pltpu.make_async_remote_copy(
            src_ref=piece(half, slot), dst_ref=piece(half, slot),
            send_sem=gather_send.at[len(sent)], recv_sem=gather_recv.at[half * 2 * line + slot],
            device_id=(peer, chan), device_id_type=MESH,
        )
        sent.append((cond, copy))
        pl.when(cond)(copy.start)

    def receive(half, slot):
        pltpu.make_async_remote_copy(
            src_ref=piece(half, slot), dst_ref=piece(half, slot),
            send_sem=gather_send.at[0], recv_sem=gather_recv.at[half * 2 * line + slot],
            device_id=(sib, chan), device_id_type=MESH,
        ).wait_recv()

    out_chan = me // per_chan

    def part_copy(other, zz, to_core):
        to = zz * 4 + x * 2 + to_core
        owner = across if other else me
        slot = 2 * zz + to_core
        place = chan * per_chan + lax.rem(owner, per_chan)
        source = partial.at[
            pl.ds(pl.multiple_of((other * 2 * line + slot) * tok, tok), tok)
        ]
        remote = pltpu.make_async_remote_copy(
            src_ref=source, dst_ref=landed.at[place],
            send_sem=part_send.at[other * 2 * line + slot], recv_sem=part_recv.at[place],
            device_id=(to, out_chan), device_id_type=MESH,
        )
        here = pltpu.make_async_copy(source, landed.at[place], part_recv.at[place])
        return to, remote, here

    def project(zz, other):
        at = pl.ds(pl.multiple_of(zz * 2 * tok, 2 * tok), 2 * tok)
        to_rows = pl.ds(pl.multiple_of((other * line + zz) * 2 * tok, 2 * tok), 2 * tok)
        weights = w_other if other else w_ref
        partial[to_rows] = jnp.dot(
            gathered[at], weights[...], preferred_element_type=F32
        ).astype(BF16)
        for to_core in range(2):
            to, remote, here = part_copy(other, zz, to_core)
            stays = jnp.logical_and(to == me, out_chan == chan)
            pl.when(stays)(here.start)
            pl.when(jnp.logical_not(stays))(remote.start)

    for half in range(2):
        send(half, 2 * z + c, me + 4, has_right)
        send(half, 2 * z + c, me - 4, has_left)
    for half in range(2):
        send(half, 2 * z + c, sib, z >= 0)
    loads[5].wait()
    for half in range(2):
        receive(half, 2 * z + 1 - c)
    project(z, 0)

    def others(last):
        for copy in w_copies:
            copy.wait_recv()
        project(z, 1)
        for d in range(1, last):
            for sign in (-1, 1):
                zz = z + sign * d
                there = zz >= 0 if sign < 0 else zz < line

                @pl.when(there)
                def _():
                    project(zz, 1)

    for d in range(1, line):
        if d == line - 1:
            others(d)
        for half in range(2):
            for sign in (-1, 1):
                zz = z + sign * d
                there = zz >= 0 if sign < 0 else zz < line
                onward = has_right if sign < 0 else has_left
                slot = 2 * zz + c

                @pl.when(there)
                def _():
                    receive(half, slot)

                send(half, slot, me - 4 * sign, jnp.logical_and(there, onward))
                send(half, slot, sib, there)
        for sign in (-1, 1):
            zz = z + sign * d
            there = zz >= 0 if sign < 0 else zz < line

            @pl.when(there)
            def _():
                for half in range(2):
                    receive(half, 2 * zz + 1 - c)
                project(zz, 0)
                if d == line - 1:
                    project(zz, 1)
    if line == 1:
        others(1)

    for i in range(per_chan):
        total = None
        for j in range(n_chan):
            slot = j * per_chan + i
            pltpu.make_async_remote_copy(
                src_ref=landed.at[slot], dst_ref=landed.at[slot],
                send_sem=part_send.at[0], recv_sem=part_recv.at[slot],
                device_id=(sib, chan), device_id_type=MESH,
            ).wait_recv()
            part = landed[slot].astype(F32)
            total = part if total is None else total + part
        out_ref[:, i * width:(i + 1) * width] = total.astype(BF16)

    for copy in end_copies + start_copies + w_copies:
        copy.wait_send()
    for cond, copy in sent:
        pl.when(cond)(copy.wait_send)
    for other in range(2):
        for slot in range(2 * line):
            to, remote, _ = part_copy(other, slot // 2, slot % 2)
            stays = jnp.logical_and(to == me, out_chan == chan)
            pl.when(jnp.logical_not(stays))(remote.wait_send)


def solution(mesh):
    n, n_chan = mesh.shape["seq"], mesh.shape["chan"]
    assert n % 4 == 0 and n % (4 * n_chan) == 0

    def body(gate_input, key_input, value_input, decay_rate, residue, skip_gain, out_weight):
        tok, chans = gate_input.shape
        modes = decay_rate.shape[0]
        width = out_weight.shape[1]
        rows = modes * chans // (LANES * n)
        hbm = pl.BlockSpec(memory_space=pltpu.HBM)
        vmem = pl.BlockSpec(memory_space=pltpu.VMEM)
        dma = pltpu.SemaphoreType.DMA
        states = pltpu.VMEM((n, rows, LANES), F32)
        return pl.pallas_call(
            functools.partial(kernel, n, n_chan),
            out_shape=jax.ShapeDtypeStruct((tok, width * (n // n_chan)), BF16),
            in_specs=[hbm] * 5 + [vmem, hbm],
            out_specs=vmem,
            scratch_shapes=[
                pltpu.VMEM((tok, chans), BF16),
                pltpu.VMEM((tok, chans), BF16),
                pltpu.VMEM((tok, chans), BF16),
                pltpu.VMEM((modes, chans), F32),
                pltpu.VMEM((modes, chans), F32),
                pltpu.VMEM((chans, width), BF16),
                pltpu.VMEM((chans, width), BF16),
                dma((6,)), dma((2,)), dma((2,)),
                pltpu.VMEM((tok, chans), F32),
                pltpu.VMEM((tok, chans), F32),
                pltpu.VMEM((tok + SUB, LANES), F32),
                states, states, states, states, states,
                pltpu.VMEM((n * tok // 2, chans), BF16),
                pltpu.VMEM((n * tok, width), BF16),
                pltpu.VMEM((n, tok, width), BF16),
                dma((n,)), dma((n,)), dma((n,)), dma((n,)),
                dma((2 * n,)), dma((n,)), dma((n,)), dma((n,)),
            ],
            compiler_params=pltpu.CompilerParams(
                collective_id=0, has_side_effects=True, vmem_limit_bytes=48 * 1024 * 1024
            ),
            cost_estimate=pl.CostEstimate(
                flops=2 * n * tok * chans * width, bytes_accessed=4 * tok * chans, transcendentals=0
            ),
        )(gate_input, key_input, value_input, decay_rate, residue,
          skip_gain.reshape(1, chans), out_weight)

    return jax.shard_map(
        body,
        mesh=mesh,
        in_specs=(
            P("seq", "chan"),
            P("seq", "chan"),
            P("seq", "chan"),
            P(None, "chan"),
            P(None, "chan"),
            P("chan"),
            P("chan", "seq"),
        ),
        out_specs=P("seq", "chan"),
        check_vma=False,
    )
```

time: 72.6 us -> 54.6 us (0.75)
  Pallas kernels: 66.7 us -> 46.6 us
  local copies, waits for them, and re-layouts: 4.53 us -> 7.28 us
  other arithmetic: 1.11 us -> 0 us
    pallas_call x1, Pallas kernels: 66.7 us -> 46.6 us  [body(): pl.pallas_call(functools.partial(kernel, n, n_chan), out_shape=jax.ShapeD...]
    unnamed x13 -> x15, local copies, waits for them, and re-layouts: 4.53 us -> 7.28 us
    mul x1 -> x0, other arithmetic: 1.11 us -> none  [body(): amplitude = residue * jnp.sqrt(-jnp.expm1(-2.0 * decay_rate))]
where the time goes in v2:
time: 54.6 us; the launch traced here: 53.9 us
  Pallas kernels  46.6 us (85%)
  local copies, waits for them, and re-layouts  7.28 us (13%)
    pallas_call x1, Pallas kernels, body(): pl.pallas_call(functools.partial(kernel, n, n_chan), out_shape=jax.ShapeD...  46.6 us
    unnamed x15, local copies, waits for them, and re-layouts  7.28 us

profile of v2, /device:TPU:7, one launch (start us, length us, event | category | flops | bytes accessed | tf_op | source)
XLA Modules:
  0.0 53.9 jit_solution(7723464927104346475)
XLA Ops:
  0.0 0.0 copy-start
  0.0 1.2 %copy-done = bf16[2048,256]{1,0:T(8,128)(2,1)S(1)} copy-done((bf16[2048,256]{1,0:T(8,128)(2,1)S(1)}, bf16[2048,256]{1,0:T(8,128)(2,1)}, u32[]{:S(2)}) %copy-start) | copy-done | bytes 1048600
  1.2 0.0 copy-start.1
  1.2 0.9 %copy-done.1 = bf16[64,2048]{1,0:T(8,128)(2,1)S(1)} copy-done((bf16[64,2048]{1,0:T(8,128)(2,1)S(1)}, bf16[64,2048]{1,0:T(8,128)(2,1)}, u32[]{:S(2)}) %copy-start.1) | copy-done | bytes 262168
  2.2 0.0 copy-start.2
  2.2 0.9 %copy-done.2 = bf16[64,2048]{1,0:T(8,128)(2,1)S(1)} copy-done((bf16[64,2048]{1,0:T(8,128)(2,1)S(1)}, bf16[64,2048]{1,0:T(8,128)(2,1)}, u32[]{:S(2)}) %copy-start.2) | copy-done | bytes 262168
  3.1 0.0 copy-start.3
  3.1 0.9 %copy-done.3 = bf16[64,2048]{1,0:T(8,128)(2,1)S(1)} copy-done((bf16[64,2048]{1,0:T(8,128)(2,1)S(1)}, bf16[64,2048]{1,0:T(8,128)(2,1)}, u32[]{:S(2)}) %copy-start.3) | copy-done | bytes 262168
  4.1 0.0 copy-start.4
  4.1 0.9 %copy-done.4 = f32[16,2048]{1,0:T(8,128)S(1)} copy-done((f32[16,2048]{1,0:T(8,128)S(1)}, f32[16,2048]{1,0:T(8,128)}, u32[]{:S(2)}) %copy-start.4) | copy-done | bytes 131096
  5.0 0.0 copy-start.5
  5.0 0.9 %copy-done.5 = f32[16,2048]{1,0:T(8,128)S(1)} copy-done((f32[16,2048]{1,0:T(8,128)S(1)}, f32[16,2048]{1,0:T(8,128)}, u32[]{:S(2)}) %copy-start.5) | copy-done | bytes 131096
  5.9 0.0 copy-start.6
  5.9 0.7 %copy-done.6 = f32[2048]{0:T(1024)S(1)} copy-done((f32[2048]{0:T(1024)S(1)}, f32[2048]{0:T(1024)}, u32[]{:S(2)}) %copy-start.6) | copy-done | bytes 8216
  6.6 46.6 %shard_map.73 = bf16[64,2048]{1,0:T(8,128)(2,1)S(1)} custom-call(bf16[64,2048]{1,0:T(8,128)(2,1)S(1)} %copy-done.1, bf16[64,2048]{1,0:T(8,128)(2,1)S(1)} %copy-done.2, bf16[64,2048]{1,0:T(8,128)(2,1)S(1)} %copy-done.3, f32[16,2048]{1,0:T(8,128)S(1)} %copy-done.4, f32[16,2048]{1,0:T(8,128)S(1)} %copy-done.5, f32[1,2048]{1,0:T(1,128)S(1)} %bitcast.1, ...), custom_call_target="tpu_custom_call" | custom-call | flops 1073741824 | bytes 524288 | tf_op jit(solution)/shard_map/pallas_call | solution.py:343
  53.2 0.7 %copy.9 = bf16[64,2048]{1,0:T(8,128)(2,1)} copy(bf16[64,2048]{1,0:T(8,128)(2,1)S(1)} %shard_map.73) | data formatting | bytes 524288
Async XLA Ops:
  0.0 1.2 %copy-start = (bf16[2048,256]{1,0:T(8,128)(2,1)S(1)}, bf16[2048,256]{1,0:T(8,128)(2,1)}, u32[]{:S(2)}) copy-start(bf16[2048,256]{1,0:T(8,128)(2,1)} %w_hbm.1) | copy-start | bytes 3145732
  1.2 0.9 %copy-start.1 = (bf16[64,2048]{1,0:T(8,128)(2,1)S(1)}, bf16[64,2048]{1,0:T(8,128)(2,1)}, u32[]{:S(2)}) copy-start(bf16[64,2048]{1,0:T(8,128)(2,1)} %q_hbm.1) | copy-start | bytes 786436
  2.2 0.9 %copy-start.2 = (bf16[64,2048]{1,0:T(8,128)(2,1)S(1)}, bf16[64,2048]{1,0:T(8,128)(2,1)}, u32[]{:S(2)}) copy-start(bf16[64,2048]{1,0:T(8,128)(2,1)} %k_hbm.1) | copy-start | bytes 786436
  3.1 0.9 %copy-start.3 = (bf16[64,2048]{1,0:T(8,128)(2,1)S(1)}, bf16[64,2048]{1,0:T(8,128)(2,1)}, u32[]{:S(2)}) copy-start(bf16[64,2048]{1,0:T(8,128)(2,1)} %v_hbm.1) | copy-start | bytes 786436
  4.1 0.9 %copy-start.4 = (f32[16,2048]{1,0:T(8,128)S(1)}, f32[16,2048]{1,0:T(8,128)}, u32[]{:S(2)}) copy-start(f32[16,2048]{1,0:T(8,128)} %rate_hbm.1) | copy-start | bytes 393220
  5.0 0.9 %copy-start.5 = (f32[16,2048]{1,0:T(8,128)S(1)}, f32[16,2048]{1,0:T(8,128)}, u32[]{:S(2)}) copy-start(f32[16,2048]{1,0:T(8,128)} %residue_hbm.1) | copy-start | bytes 393220
  5.9 0.7 %copy-start.6 = (f32[2048]{0:T(1024)S(1)}, f32[2048]{0:T(1024)}, u32[]{:S(2)}) copy-start(f32[2048]{0:T(1024)} %param.12) | copy-start | bytes 24580

commit v3 on v2

--- a/solution.py
+++ b/solution.py
@@ -87,7 +87,7 @@
         state = jnp.concatenate(found, axis=0)
         fade = jnp.exp(-float(tok) * rate_ref[:, at])
         for p in range(per_block):
-            ends[b * per_block + p] = state[p * rows:(p + 1) * rows]
+            ends[b * per_block + p] = state[p * rows:(p + 1) * rows].astype(BF16)
             fades[b * per_block + p] = fade[p * rows:(p + 1) * rows]
         return 0
 
@@ -118,7 +118,23 @@
                 device_id=(peer, chan), device_id_type=MESH,
             ).wait_recv()
 
+    across = me + 2 - 4 * x
+    w_copies = []
+    w_rows = chans // 8
+
+    def swap(first, last):
+        for part in range(first, last):
+            at = pl.ds(part * w_rows, w_rows)
+            copy = pltpu.make_async_remote_copy(
+                src_ref=w_hbm.at[at], dst_ref=w_other.at[at],
+                send_sem=w_send.at[part], recv_sem=w_recv.at[part],
+                device_id=(across, chan), device_id_type=MESH,
+            )
+            copy.start()
+            w_copies.append(copy)
+
     end_copies = exchange(ends, ends_all, end_send, end_recv)
+    swap(0, 1)
 
     loads[3].wait()
     amp_ref[...] = amp_ref[...] * jnp.sqrt(one_minus_exp(2.0 * rate_ref[...]))
@@ -155,22 +171,11 @@
     fade = fades[me]
     state = jnp.zeros((rows, LANES), F32)
     for i in range(n):
-        starts_all[i] = state
+        starts_all[i] = state.astype(BF16)
         if i < n - 1:
-            state = state * fade + ends_all[i]
+            state = state * fade + ends_all[i].astype(F32)
     start_copies = exchange(starts_all, starts, start_send, start_recv)
-    across = me + 2 - 4 * x
-    w_copies = []
-    w_rows = chans // 2
-    for half in range(2):
-        at = pl.ds(half * w_rows, w_rows)
-        copy = pltpu.make_async_remote_copy(
-            src_ref=w_hbm.at[at], dst_ref=w_other.at[at],
-            send_sem=w_send.at[half], recv_sem=w_recv.at[half],
-            device_id=(across, chan), device_id_type=MESH,
-        )
-        copy.start()
-        w_copies.append(copy)
+    swap(1, 8)
     loads[4].wait()
     arrivals(starts, start_send, start_recv)
 
@@ -178,11 +183,12 @@
 
     def gate_block(b, _):
         at = lanes(b)
+        held = [starts[b * per_block + p].astype(F32) for p in range(per_block)]
         totals = [local[t * SUB:(t + 1) * SUB, at] for t in range(tiles)]
         for m in range(modes):
             rate = rate_ref[pl.ds(m, 1), at]
             jump = jnp.exp(-float(SUB) * rate)
-            start = starts[b * per_block + m // rows][m % rows:m % rows + 1]
+            start = held[m // rows][m % rows:m % rows + 1]
             term = (amp_ref[pl.ds(m, 1), at] * start) * jnp.exp(-rate * (steps + 1.0))
             for t in range(tiles):
                 totals[t] = totals[t] + term
@@ -192,16 +198,17 @@
         gathered[pl.ds(own_rows, tok), at] = gated.astype(BF16)
         return 0
 
-    lax.fori_loop(0, blocks, gate_block, 0)
-
-    half_rows = tok // 2
+
+    half_cols = chans // 2
     sib = me + 1 - 2 * c
     has_right = z < line - 1
     has_left = z > 0
     sent = []
 
     def piece(half, slot):
-        return gathered.at[pl.ds(pl.multiple_of(slot * tok + half * half_rows, half_rows), half_rows)]
+        return gathered.at[
+            pl.ds(pl.multiple_of(slot * tok, tok), tok), pl.ds(half * half_cols, half_cols)
+        ]
 
     def send(half, slot, peer, cond):
         copy = pltpu.make_async_remote_copy(
@@ -251,9 +258,9 @@
             pl.when(jnp.logical_not(stays))(remote.start)
 
     for half in range(2):
+        lax.fori_loop(half * blocks // 2, (half + 1) * blocks // 2, gate_block, 0)
         send(half, 2 * z + c, me + 4, has_right)
         send(half, 2 * z + c, me - 4, has_left)
-    for half in range(2):
         send(half, 2 * z + c, sib, z >= 0)
     loads[5].wait()
     for half in range(2):
@@ -339,7 +346,7 @@
         hbm = pl.BlockSpec(memory_space=pltpu.HBM)
         vmem = pl.BlockSpec(memory_space=pltpu.VMEM)
         dma = pltpu.SemaphoreType.DMA
-        states = pltpu.VMEM((n, rows, LANES), F32)
+        states = pltpu.VMEM((n, rows, LANES), BF16)
         return pl.pallas_call(
             functools.partial(kernel, n, n_chan),
             out_shape=jax.ShapeDtypeStruct((tok, width * (n // n_chan)), BF16),
@@ -353,11 +360,12 @@
                 pltpu.VMEM((modes, chans), F32),
                 pltpu.VMEM((chans, width), BF16),
                 pltpu.VMEM((chans, width), BF16),
-                dma((6,)), dma((2,)), dma((2,)),
+                dma((6,)), dma((8,)), dma((8,)),
                 pltpu.VMEM((tok, chans), F32),
                 pltpu.VMEM((tok, chans), F32),
                 pltpu.VMEM((tok + SUB, LANES), F32),
-                states, states, states, states, states,
+                pltpu.VMEM((n, rows, LANES), F32),
+                states, states, states, states,
                 pltpu.VMEM((n * tok // 2, chans), BF16),
                 pltpu.VMEM((n * tok, width), BF16),
                 pltpu.VMEM((n, tok, width), BF16),
@@ -365,7 +373,7 @@
                 dma((2 * n,)), dma((n,)), dma((n,)), dma((n,)),
             ],
             compiler_params=pltpu.CompilerParams(
-                collective_id=0, has_side_effects=True, vmem_limit_bytes=48 * 1024 * 1024
+                collective_id=0, has_side_effects=True, vmem_limit_bytes=67043328
             ),
             cost_estimate=pl.CostEstimate(
                 flops=2 * n * tok * chans * width, bytes_accessed=4 * tok * chans, transcendentals=0

time: 54.6 us -> 47.7 us (0.87)
  local copies, waits for them, and re-layouts: 7.28 us -> 1.67 us
  Pallas kernels: 46.6 us -> 45.8 us
    unnamed x15 -> x1, local copies, waits for them, and re-layouts: 7.28 us -> 1.67 us
    pallas_call x1, Pallas kernels: 46.6 us -> 45.8 us  [body(): pl.pallas_call(functools.partial(kernel, n, n_chan), out_shape=jax.ShapeD...]
where the time goes in v3:
time: 47.7 us; the launch traced here: 47.5 us
  Pallas kernels  45.8 us (96%)
  local copies, waits for them, and re-layouts  1.67 us (4%)
    pallas_call x1, Pallas kernels, body(): pl.pallas_call(functools.partial(kernel, n, n_chan), out_shape=jax.ShapeD...  45.8 us
    unnamed x1, local copies, waits for them, and re-layouts  1.67 us

profile of v3, /device:TPU:7, one launch (start us, length us, event | category | flops | bytes accessed | tf_op | source)
XLA Modules:
  0.0 47.5 jit_solution(1182981485226774843)
XLA Ops:
  0.0 45.8 %shard_map.73 = bf16[64,2048]{1,0:T(8,128)(2,1)} custom-call(bf16[64,2048]{1,0:T(8,128)(2,1)} %q_hbm.1, bf16[64,2048]{1,0:T(8,128)(2,1)} %k_hbm.1, bf16[64,2048]{1,0:T(8,128)(2,1)} %v_hbm.1, f32[16,2048]{1,0:T(8,128)} %rate_hbm.1, f32[16,2048]{1,0:T(8,128)} %residue_hbm.1, f32[1,2048]{1,0:T(1,128)} %bitcast.1, bf16[2048,256]{1,0:T(8,128)(2,1)} %w_hbm.1), custom_call_target="tpu_custom_call" | custom-call | flops 1073741824 | bytes 524288 | tf_op jit(solution)/shard_map/pallas_call | solution.py:350
  45.8 1.7 %copy.9 = bf16[64,2048]{1,0:T(8,128)(2,1)} copy(bf16[64,2048]{1,0:T(8,128)(2,1)} %shard_map.73) | data formatting | bytes 524288

commit v4 on v3

--- a/solution.py
+++ b/solution.py
@@ -97,7 +97,7 @@
 
     def exchange(source, target, send_sem, recv_sem):
         copies = []
-        for hop in range(1, n):
+        for hop in sorted(range(1, n), key=lambda h: abs(h - n // 2)):
             peer = lax.rem(me + hop, n)
             copy = pltpu.make_async_remote_copy(
                 src_ref=source.at[peer], dst_ref=target.at[me],

time: 47.7 us -> 47.5 us (level)
  no operation moved by 1% of the time
where the time goes in v4:
time: 47.5 us; the launch traced here: 47.2 us
  Pallas kernels  45.6 us (96%)
  local copies, waits for them, and re-layouts  1.67 us (4%)
    pallas_call x1, Pallas kernels, body(): pl.pallas_call(functools.partial(kernel, n, n_chan), out_shape=jax.ShapeD...  45.6 us
    unnamed x1, local copies, waits for them, and re-layouts  1.67 us

profile of v4, /device:TPU:7, one launch (start us, length us, event | category | flops | bytes accessed | tf_op | source)
XLA Modules:
  0.0 47.2 jit_solution(931469507882042555)
XLA Ops:
  0.0 45.6 %shard_map.73 = bf16[64,2048]{1,0:T(8,128)(2,1)} custom-call(bf16[64,2048]{1,0:T(8,128)(2,1)} %q_hbm.1, bf16[64,2048]{1,0:T(8,128)(2,1)} %k_hbm.1, bf16[64,2048]{1,0:T(8,128)(2,1)} %v_hbm.1, f32[16,2048]{1,0:T(8,128)} %rate_hbm.1, f32[16,2048]{1,0:T(8,128)} %residue_hbm.1, f32[1,2048]{1,0:T(1,128)} %bitcast.1, bf16[2048,256]{1,0:T(8,128)(2,1)} %w_hbm.1), custom_call_target="tpu_custom_call" | custom-call | flops 1073741824 | bytes 524288 | tf_op jit(solution)/shard_map/pallas_call | solution.py:350
  45.6 1.7 %copy.9 = bf16[64,2048]{1,0:T(8,128)(2,1)} copy(bf16[64,2048]{1,0:T(8,128)(2,1)} %shard_map.73) | data formatting | bytes 524288
